TPU v7x, 32 devices: a whole 2x2x4 slice. The times are simulated.
32 devices in a mesh: seq: 4 (over z), shard: 8 (over y, x, core).
Axes of the slice: x: 2, y: 2, z: 4, core: 2. Of those that a mesh axis runs over, the one named last changes fastest.
Arguments:
- tokens: bfloat16 [8, 2048, 1024], P('shard', 'seq'), may hold values from -6 to 6
- ln1_gain: bfloat16 [1024], P(('seq', 'shard')), may hold values from 0.5 to 1.5
- ln1_bias: bfloat16 [1024], P(('seq', 'shard')), may hold values from -3 to 3
- w_qkv: bfloat16 [1024, 3072], P(('seq', 'shard')), may hold values from -0.1875 to 0.1875
- bias_query: bfloat16 [1024], P(('seq', 'shard')), may hold values from -3 to 3
- bias_value: bfloat16 [1024], P(('seq', 'shard')), may hold values from -3 to 3
- w_out: bfloat16 [1024, 1024], P(('seq', 'shard')), may hold values from -1 to 1
- bias_out: bfloat16 [1024], P(('seq', 'shard')), may hold values from -3 to 3
- ln2_gain: bfloat16 [1024], P(('seq', 'shard')), may hold values from 0.5 to 1.5
- ln2_bias: bfloat16 [1024], P(('seq', 'shard')), may hold values from -3 to 3
- w_in: bfloat16 [1024, 4096], P(('seq', 'shard')), may hold values from -0.1875 to 0.1875
- bias_in: bfloat16 [4096], P(('seq', 'shard')), may hold values from -3 to 3
- w_back: bfloat16 [4096, 1024], P(('seq', 'shard')), may hold values from -0.09375 to 0.09375
- bias_back: bfloat16 [1024], P(('seq', 'shard')), may hold values from -3 to 3
- cotangent: bfloat16 [8, 2048, 1024], P('shard', 'seq'), may hold values from -6 to 6
Outputs:
- result: bfloat16 [8, 2048, 1024], P('shard', 'seq')
- grad_tokens: float32 [8, 2048, 1024], P('shard', 'seq')
- grad_ln1_gain: float32 [1024], P(('seq', 'shard'))
- grad_ln1_bias: float32 [1024], P(('seq', 'shard'))
- grad_w_qkv: float32 [1024, 3072], P(('seq', 'shard'))
- grad_bias_query: float32 [1024], P(('seq', 'shard'))
- grad_bias_value: float32 [1024], P(('seq', 'shard'))
- grad_w_out: float32 [1024, 1024], P(('seq', 'shard'))
- grad_bias_out: float32 [1024], P(('seq', 'shard'))
- grad_ln2_gain: float32 [1024], P(('seq', 'shard'))
- grad_ln2_bias: float32 [1024], P(('seq', 'shard'))
- grad_w_in: float32 [1024, 4096], P(('seq', 'shard'))
- grad_bias_in: float32 [4096], P(('seq', 'shard'))
- grad_w_back: float32 [4096, 1024], P(('seq', 'shard'))
- grad_bias_back: float32 [1024], P(('seq', 'shard'))
All inputs are finite; a program needn't handle non-finite values.
Results may differ from a plain program's by a relative error of at most 0.014.
The roundings to bfloat16 on the way count: a program that leaves them out, or rounds other values in their place, can miss the bound.
Values may be sent and summed in bfloat16 or wider, within the bound.
A program may use at most 192 MiB of HBM per device.

v0:
```python
import math
import jax
import jax.numpy as jnp
from jax import lax
from jax.sharding import PartitionSpec as P

HEAD_DIM = 64
norm_eps = 1e-05
gelu_c = math.sqrt(2.0 / math.pi)


def normalize(values):
    mean_row = jnp.mean(values, axis=-1, keepdims=True)
    centred = values - mean_row
    var_row = jnp.mean(centred * centred, axis=-1, keepdims=True)
    scale_row = lax.rsqrt(var_row + norm_eps)
    return (centred * scale_row, scale_row)


def norm_back(dnormed, normed, scale_row):
    return scale_row * (
        dnormed
        - jnp.mean(dnormed, axis=-1, keepdims=True)
        - normed * jnp.mean(dnormed * normed, axis=-1, keepdims=True)
    )


def gelu_pair(inputs):
    inner = gelu_c * (inputs + 0.044715 * inputs * inputs * inputs)
    tanh_val = jnp.tanh(inner)
    value = 0.5 * inputs * (1.0 + tanh_val)
    slope = 0.5 * (1.0 + tanh_val) + 0.5 * inputs * (1.0 - tanh_val * tanh_val) * gelu_c * (
        1.0 + 3.0 * 0.044715 * inputs * inputs
    )
    return (value, slope)


def masked_scores(query_block, keys, start, scale):
    block = query_block.shape[0]
    length = keys.shape[0]
    scores = (
        jnp.einsum("qgd,kgd->gqk", query_block, keys, preferred_element_type=jnp.float32) * scale
    )
    q_pos = start + jnp.arange(block, dtype=jnp.int32)
    k_pos = jnp.arange(length, dtype=jnp.int32)
    allowed = k_pos[None, None, :] <= q_pos[None, :, None]
    return jnp.where(allowed, scores, -1e30)


def attend_forward(query, keys, values):
    length, groups, width = query.shape
    block = min(512, length)
    scale = 1.0 / math.sqrt(width)

    def one_block(index):
        start = index * block
        q_blk = lax.dynamic_slice_in_dim(query, start, block, 0)
        scores = masked_scores(q_blk, keys, start, scale)
        log_total = jnp.log(jnp.sum(jnp.exp(scores), axis=-1))
        probs = jnp.exp(scores - log_total[:, :, None]).astype(jnp.bfloat16)
        attended = jnp.einsum("gqk,kgd->qgd", probs, values, preferred_element_type=jnp.float32)
        return (attended.astype(jnp.bfloat16), log_total)

    outs, logs = lax.map(one_block, jnp.arange(length // block, dtype=jnp.int32))
    return (outs.reshape(length, groups, width), logs)


def attend_backward(query, keys, values, attended, logs, d_att):
    length, groups, width = query.shape
    block = min(512, length)
    scale = 1.0 / math.sqrt(width)

    def one_block(carry, index):
        d_keys, d_values = carry
        start = index * block
        q_blk = lax.dynamic_slice_in_dim(query, start, block, 0)
        o_blk = lax.dynamic_slice_in_dim(attended, start, block, 0)
        do_blk = lax.dynamic_slice_in_dim(d_att, start, block, 0)
        scores = masked_scores(q_blk, keys, start, scale)
        log_total = lax.dynamic_index_in_dim(logs, index, 0, keepdims=False)
        probs = jnp.exp(scores - log_total[:, :, None])
        probs_b = probs.astype(jnp.bfloat16)
        d_values = d_values + jnp.einsum(
            "gqk,qgd->kgd", probs_b, do_blk, preferred_element_type=jnp.float32
        )
        d_probs = jnp.einsum("qgd,kgd->gqk", do_blk, values, preferred_element_type=jnp.float32)
        delta = jnp.swapaxes(
            jnp.sum(do_blk.astype(jnp.float32) * o_blk.astype(jnp.float32), axis=-1), 0, 1
        )
        d_scores = (probs * (d_probs - delta[:, :, None]) * scale).astype(jnp.bfloat16)
        d_query = jnp.einsum(
            "gqk,kgd->qgd", d_scores, keys, preferred_element_type=jnp.float32
        ).astype(jnp.bfloat16)
        d_keys = d_keys + jnp.einsum(
            "gqk,qgd->kgd", d_scores, q_blk, preferred_element_type=jnp.float32
        )
        return ((d_keys, d_values), d_query)

    zeros = jnp.zeros((length, groups, width), jnp.float32)
    (d_keys, d_values), d_queries = lax.scan(
        one_block, (zeros, zeros), jnp.arange(length // block, dtype=jnp.int32)
    )
    return (
        d_queries.reshape(length, groups, width),
        d_keys.astype(jnp.bfloat16),
        d_values.astype(jnp.bfloat16),
    )


def col_dot(left, right):
    return lax.dot_general(
        left, right, (((0,), (0,)), ((), ())), preferred_element_type=jnp.float32
    )


def row_dot(left, right):
    return lax.dot_general(
        left, right, (((1,), (1,)), ((), ())), preferred_element_type=jnp.float32
    )


def per_device(
    tokens,
    ln1_gain,
    ln1_bias,
    w_qkv,
    bias_query,
    bias_value,
    w_out,
    bias_out,
    ln2_gain,
    ln2_bias,
    w_in,
    bias_in,
    w_back,
    bias_back,
    cotangent,
):
    f32 = jnp.float32
    params = (
        lax.all_gather(ln1_gain, ("seq", "shard"), axis=0, tiled=True),
        lax.all_gather(ln1_bias, ("seq", "shard"), axis=0, tiled=True),
        lax.all_gather(w_qkv, ("seq", "shard"), axis=0, tiled=True),
        lax.all_gather(bias_query, ("seq", "shard"), axis=0, tiled=True),
        lax.all_gather(bias_value, ("seq", "shard"), axis=0, tiled=True),
        lax.all_gather(w_out, ("seq", "shard"), axis=0, tiled=True),
        lax.all_gather(bias_out, ("seq", "shard"), axis=0, tiled=True),
        lax.all_gather(ln2_gain, ("seq", "shard"), axis=0, tiled=True),
        lax.all_gather(ln2_bias, ("seq", "shard"), axis=0, tiled=True),
        lax.all_gather(w_in, ("seq", "shard"), axis=0, tiled=True),
        lax.all_gather(bias_in, ("seq", "shard"), axis=0, tiled=True),
        lax.all_gather(w_back, ("seq", "shard"), axis=0, tiled=True),
        lax.all_gather(bias_back, ("seq", "shard"), axis=0, tiled=True),
    )
    (
        g_one,
        s_one,
        full_qkv,
        full_bq,
        full_bv,
        full_out,
        full_bo,
        g_two,
        s_two,
        full_in,
        full_bin,
        full_back,
        full_bback,
    ) = params
    rows = tokens.shape[1]
    width = tokens.shape[2]
    x_f = tokens[0].astype(f32)
    normed1, scale1 = normalize(x_f)
    h_one = (normed1 * g_one.astype(f32) + s_one.astype(f32)).astype(jnp.bfloat16)
    bias_qkv = jnp.concatenate([full_bq.astype(f32), jnp.zeros((width,), f32), full_bv.astype(f32)])
    qkv = (jnp.dot(h_one, full_qkv, preferred_element_type=f32) + bias_qkv).astype(jnp.bfloat16)
    grouped = lax.all_to_all(
        qkv.reshape(rows, 3, width), "seq", split_axis=2, concat_axis=0, tiled=True
    )
    length = grouped.shape[0]
    local_width = grouped.shape[2]
    groups = local_width // HEAD_DIM
    query = grouped[:, 0].reshape(length, groups, HEAD_DIM)
    keys = grouped[:, 1].reshape(length, groups, HEAD_DIM)
    values = grouped[:, 2].reshape(length, groups, HEAD_DIM)
    attended, logs = attend_forward(query, keys, values)
    att_tok = lax.all_to_all(
        attended.reshape(length, local_width), "seq", split_axis=0, concat_axis=1, tiled=True
    )
    resid = x_f + jnp.dot(att_tok, full_out, preferred_element_type=f32) + full_bo.astype(f32)
    normed2, scale2 = normalize(resid)
    h_two = (normed2 * g_two.astype(f32) + s_two.astype(f32)).astype(jnp.bfloat16)
    pre = jnp.dot(h_two, full_in, preferred_element_type=f32) + full_bin.astype(f32)
    act_val, slope = gelu_pair(pre)
    act = act_val.astype(jnp.bfloat16)
    result = (
        resid + jnp.dot(act, full_back, preferred_element_type=f32) + full_bback.astype(f32)
    ).astype(jnp.bfloat16)
    cot_b = cotangent[0]
    cot_f = cot_b.astype(f32)
    g_w_back = col_dot(act, cot_b)
    g_b_back = jnp.sum(cot_f, axis=0)
    d_pre = (row_dot(cot_b, full_back) * slope).astype(jnp.bfloat16)
    g_w_in = col_dot(h_two, d_pre)
    g_b_in = jnp.sum(d_pre.astype(f32), axis=0)
    d_h2 = row_dot(d_pre, full_in)
    g_g2 = jnp.sum(d_h2 * normed2, axis=0)
    g_s2 = jnp.sum(d_h2, axis=0)
    d_resid = cot_f + norm_back(d_h2 * g_two.astype(f32), normed2, scale2)
    d_resid_b = d_resid.astype(jnp.bfloat16)
    g_w_out = col_dot(att_tok, d_resid_b)
    g_b_out = jnp.sum(d_resid, axis=0)
    d_att_tok = row_dot(d_resid_b, full_out).astype(jnp.bfloat16)
    d_att = lax.all_to_all(d_att_tok, "seq", split_axis=1, concat_axis=0, tiled=True).reshape(
        length, groups, HEAD_DIM
    )
    d_query, d_keys, d_values = attend_backward(query, keys, values, attended, logs, d_att)
    stacked = jnp.stack(
        [
            d_query.reshape(length, local_width),
            d_keys.reshape(length, local_width),
            d_values.reshape(length, local_width),
        ],
        axis=1,
    )
    d_qkv = lax.all_to_all(stacked, "seq", split_axis=0, concat_axis=2, tiled=True).reshape(
        rows, 3 * width
    )
    g_w_qkv = col_dot(h_one, d_qkv)
    g_bq = jnp.sum(d_qkv[:, :width].astype(f32), axis=0)
    g_bv = jnp.sum(d_qkv[:, 2 * width :].astype(f32), axis=0)
    d_h1 = row_dot(d_qkv, full_qkv)
    g_g1 = jnp.sum(d_h1 * normed1, axis=0)
    g_s1 = jnp.sum(d_h1, axis=0)
    d_tokens = d_resid + norm_back(d_h1 * g_one.astype(f32), normed1, scale1)
    summed = (
        lax.psum_scatter(g_g1, ("seq", "shard"), scatter_dimension=0, tiled=True),
        lax.psum_scatter(g_s1, ("seq", "shard"), scatter_dimension=0, tiled=True),
        lax.psum_scatter(g_w_qkv, ("seq", "shard"), scatter_dimension=0, tiled=True),
        lax.psum_scatter(g_bq, ("seq", "shard"), scatter_dimension=0, tiled=True),
        lax.psum_scatter(g_bv, ("seq", "shard"), scatter_dimension=0, tiled=True),
        lax.psum_scatter(g_w_out, ("seq", "shard"), scatter_dimension=0, tiled=True),
        lax.psum_scatter(g_b_out, ("seq", "shard"), scatter_dimension=0, tiled=True),
        lax.psum_scatter(g_g2, ("seq", "shard"), scatter_dimension=0, tiled=True),
        lax.psum_scatter(g_s2, ("seq", "shard"), scatter_dimension=0, tiled=True),
        lax.psum_scatter(g_w_in, ("seq", "shard"), scatter_dimension=0, tiled=True),
        lax.psum_scatter(g_b_in, ("seq", "shard"), scatter_dimension=0, tiled=True),
        lax.psum_scatter(g_w_back, ("seq", "shard"), scatter_dimension=0, tiled=True),
        lax.psum_scatter(g_b_back, ("seq", "shard"), scatter_dimension=0, tiled=True),
    )
    (
        r_g1,
        r_s1,
        r_w_qkv,
        r_bq,
        r_bv,
        r_w_out,
        r_b_out,
        r_g2,
        r_s2,
        r_w_in,
        r_b_in,
        r_w_back,
        r_b_back,
    ) = summed
    return (
        result[None],
        d_tokens[None],
        r_g1,
        r_s1,
        r_w_qkv,
        r_bq,
        r_bv,
        r_w_out,
        r_b_out,
        r_g2,
        r_s2,
        r_w_in,
        r_b_in,
        r_w_back,
        r_b_back,
    )


def solution(mesh):
    return jax.shard_map(
        per_device,
        mesh=mesh,
        in_specs=(
            P("shard", "seq", None),
            P(("seq", "shard")),
            P(("seq", "shard")),
            P(("seq", "shard"), None),
            P(("seq", "shard")),
            P(("seq", "shard")),
            P(("seq", "shard"), None),
            P(("seq", "shard")),
            P(("seq", "shard")),
            P(("seq", "shard")),
            P(("seq", "shard"), None),
            P(("seq", "shard")),
            P(("seq", "shard"), None),
            P(("seq", "shard")),
            P("shard", "seq", None),
        ),
        out_specs=(
            P("shard", "seq", None),
            P("shard", "seq", None),
            P(("seq", "shard")),
            P(("seq", "shard")),
            P(("seq", "shard"), None),
            P(("seq", "shard")),
            P(("seq", "shard")),
            P(("seq", "shard"), None),
            P(("seq", "shard")),
            P(("seq", "shard")),
            P(("seq", "shard")),
            P(("seq", "shard"), None),
            P(("seq", "shard")),
            P(("seq", "shard"), None),
            P(("seq", "shard")),
        ),
        check_vma=False,
    )
```

profile of v0, /device:TPU:13, one launch (start us, length us, event | category | flops | bytes accessed | tf_op | source)
XLA Modules:
  0.0 1236.6 jit_solution(11690931587588916261)
XLA Ops:
  16.1 40.8 %all-reduce.18 = (bf16[1024]{0:T(1024)(128)(2,1)S(1)}, bf16[1024]{0:T(1024)(128)(2,1)S(1)}, bf16[1024]{0:T(1024)(128)(2,1)S(1)}, bf16[1024]{0:T(1024)(128)(2,1)S...) all-reduce(bf16[1024]{0:T(1024)(128)(2,1)S(1)} %dynamic-update-slic, ...), channel_id=1, replica_groups=mesh['seq'=4,'shard'=8] {'seq','shard'}, use_global_device_ids=true, to_apply=%add.3 | all-reduce | flops 8192 | bytes 32768
  60.1 21.6 %all-gather.6.cloned.1.call-done = bf16[1024,3072]{1,0:T(8,128)(2,1)} async-done(((bf16[32,3072]{1,0:T(8,128)(2,1)}), bf16[1024,3072]{1,0:T(8,128)(2,1)}) %all-gather.6.cloned.1.call-update) | async-done | bytes 6291472 | tf_op jit(solution)/shard_map/all_gather | solution.py:143
  103.5 101.0 %all-to-all-done = bf16[512,3,1024]{0,1,2:T(4,128)(2,1)} async-done(((bf16[512,3,1024]{0,1,2:T(4,128)(2,1)}), bf16[512,3,1024]{0,1,2:T(4,128)(2,1)}, u32[]{:S(2)}, u32[]{:S(2)}) %all-to-all-start) | async-done | bytes 3145760 | tf_op jit(solution)/shard_map/all_to_all | solution.py:177
  216.3 50.8 %while.27 = (s32[]{:T(128)}, bf16[4,512,4,64]{1,3,2,0:T(8,128)(2,1)}, f32[4,4,512]{2,1,0:T(4,128)}, s32[4]{0:T(128)S(1)}, bf16[2048,4,64]{0,2,1:T(8,128)(2,1)S(1...) while((s32[]{:T(128)}, ...), condition=%wide.region_4.5_spmd, body=%wide.region_2.4_spmd.sunk | while | flops 1104280064 | bytes 43569372 | solution.py:64
  275.6 54.4 %all-gather = bf16[32,1,128]{2,1,0:T(2,128)(2,1)S(1)} all-gather(bf16[1,1,128]{2,1,0:T(2,128)(2,1)S(1)} %bitcast.188), channel_id=1, replica_groups=mesh['seq'=4,'shard'=8] {'seq','shard'}, dimensions={0}, use_global_device_ids=true | all-gather | bytes 8448 | tf_op jit(solution)/shard_map/all_gather | solution.py:151
  335.1 10.6 fusion.83
  345.7 11.9 all-gather.12.cloned.1.call-done
  357.6 14.9 %convert_reduce_fusion = (f32[4096]{0:T(1024)}, bf16[512,4096]{1,0:T(8,128)(2,1)}) fusion(f32[512,4096]{1,0:T(8,128)} %fusion.83, f32[4096]{0:T(1024)S(1)} %bitcast.185, bf16[4096,1024]{1,0:T(8,128)(2,1)} %all-gather.12.cloned.1.call-done, bf16[1,512,1024]{2,1,0:T(8,128)(2,1)} %param.33), kind=kOutput, calls=%fused_computation.52 | convolution fusion | flops 4341100544 | bytes 22052864 | tf_op jit(solution)/shard_map/dot_general | solution.py:117
  397.3 15.6 %all-to-all-done.2 = bf16[512,4,256]{2,0,1:T(8,128)(2,1)} async-done(((bf16[512,4,256]{2,0,1:T(8,128)(2,1)}), bf16[512,4,256]{2,0,1:T(8,128)(2,1)}, u32[]{:S(2)}, u32[]{:S(2)}) %all-to-all-start.2) | async-done | bytes 1048608 | tf_op jit(solution)/shard_map/all_to_all | solution.py:214
  416.7 156.1 %while.28 = (s32[]{:T(128)}, f32[2048,4,64]{0,2,1:T(8,128)}, f32[2048,4,64]{0,2,1:T(8,128)}, bf16[4,512,4,64]{1,3,2,0:T(8,128)(2,1)}, s32[4]{0:T(128)S(1)}, /*in...) while((s32[]{:T(128)}, f32[2048,4,64]{0,2,1:T(8,128)}, ...), condition=%wide.region_11.12_spmd.clone, body=%wide.region_9.11_spmd.clone.sunk | while | flops 2734291456 | bytes 138236336 | solution.py:100
  433.4 10.5 multiply_convert_fusion.5
  471.9 10.5 multiply_convert_fusion.5
  511.0 10.5 multiply_convert_fusion.5
  550.1 10.5 multiply_convert_fusion.5
  583.7 97.2 %all_to_all.68 = bf16[2048,3,256]{2,1,0:T(4,128)(2,1)S(1)} all-to-all(bf16[2048,3,256]{2,1,0:T(4,128)(2,1)} %copy.82), channel_id=1, replica_groups=mesh['seq'=4,'shard'=8] {'seq'}, dimensions={0} | all-to-all | bytes 6291456 | tf_op jit(solution)/shard_map/all_to_all | solution.py:226
  687.8 8.7 fusion.65
  697.7 16.2 %fusion.68 = f32[4096,1024]{1,0:T(8,128)} fusion(bf16[1,512,1024]{2,1,0:T(8,128)(2,1)S(1)} %copy-done.16, f32[512,4096]{1,0:T(8,128)} %fusion.83, f32[4096]{0:T(1024)S(1)} %bitcast.186), kind=kOutput, calls=%fused_computation.98 | convolution fusion | flops 4315938816 | bytes 26230784 | tf_op jit(solution)/shard_map/dot_general | solution.py:111
  715.7 11.5 fusion.82
  727.8 13.2 %fusion.63 = bf16[1,512,1024]{2,1,0:T(8,128)(2,1)} fusion(f32[512,1024]{1,0:T(8,128)S(1)} %copy-done.6, bf16[4096,1024]{1,0:T(8,128)(2,1)} %all-gather.12.cloned.1.call-done, f32[1024]{0:T(1024)S(1)} %convert_element_type.124, f32[512,4096]{1,0:T(8,128)} %fusion.83, f32[4096]{0:T(1024)S(1)} %bitcast.187), kind=kOutput, calls=%fused_computation.94 | convolution fusion | flops 4317511680 | bytes 19943424 | tf_op jit(solution)/shard_map/dot_general | solution.py:197
  741.5 8.8 fusion.56
  750.3 45.6 %all-reduce.17 = (f32[1024]{0:T(1024)S(1)}, f32[1024]{0:T(1024)S(1)}, f32[1024]{0:T(1024)S(1)}, f32[1024]{0:T(1024)S(1)}, f32[1024]{0:T(1024)S(1)}, /*index=5*/f...) all-reduce(f32[1024]{0:T(1024)S(1)} %get-tuple-element.184, ...), channel_id=2, replica_groups=mesh['seq'=4,'shard'=8] {'seq','shard'}, use_global_device_ids=true, to_apply=%region_15.16.clone | all-reduce | flops 12288 | bytes 98304
  804.8 48.2 %reduce-scatter.5.cloned.1.call-done = f32[32,3072]{1,0:T(8,128)} async-done(((f32[1024,3072]{1,0:T(8,128)}), f32[32,3072]{1,0:T(8,128)}) %reduce-scatter.5.cloned.1.call-update) | async-done | bytes 393232 | tf_op jit(solution)/shard_map/reduce_scatter | solution.py:239
  853.0 189.0 %reduce-scatter.11.cloned.1.call-done = f32[128,1024]{1,0:T(8,128)} async-done(((f32[4096,1024]{1,0:T(8,128)}), f32[128,1024]{1,0:T(8,128)}) %reduce-scatter.11.cloned.1.call-update) | async-done | bytes 524304 | tf_op jit(solution)/shard_map/reduce_scatter | solution.py:248
  1042.1 187.5 %reduce-scatter.9.cloned.1.call-done = f32[32,4096]{1,0:T(8,128)} async-done(((f32[1024,4096]{1,0:T(8,128)}), f32[32,4096]{1,0:T(8,128)}) %reduce-scatter.9.cloned.1.call-update) | async-done | bytes 524304 | tf_op jit(solution)/shard_map/reduce_scatter | solution.py:246
  (294 shorter events, 269.0 us)
Async XLA Ops:
  7.2 74.5 %all-gather.6.cloned.1.call-start = ((), (), s32[]{:S(2)}) async-start(), calls=%async_computation.8 | async-start | bytes 6488064 | tf_op jit(solution)/shard_map/all_gather | solution.py:143
  7.9 322.1 %all-gather.8.cloned.1.call-start = ((), (), s32[]{:S(2)}) async-start(), calls=%async_computation.9 | async-start | bytes 2162688 | tf_op jit(solution)/shard_map/all_gather | solution.py:146
  8.7 326.5 %all-gather.10.cloned.1.call-start = ((), (), s32[]{:S(2)}) async-start(), calls=%async_computation.10 | async-start | bytes 8650752 | tf_op jit(solution)/shard_map/all_gather | solution.py:150
  56.9 24.8 %copy-start.25 = (f32[1024]{0:T(1024)}, f32[1024]{0:T(1024)S(1)}, u32[]{:S(2)}) copy-start(f32[1024]{0:T(1024)S(1)} %convert_element_type.112) | copy-start | bytes 12292
  56.9 24.8 %copy-start.38 = (f32[1024]{0:T(1024)}, f32[1024]{0:T(1024)S(1)}, u32[]{:S(2)}) copy-start(f32[1024]{0:T(1024)S(1)} %convert_element_type.113) | copy-start | bytes 12292
  58.4 23.3 %copy-start.21 = (f32[512]{0:T(512)}, f32[512]{0:T(512)S(1)}, u32[]{:S(2)}) copy-start(f32[512]{0:T(512)S(1)} %broadcast_multiply_fusion.5) | copy-start | bytes 6148
  60.1 21.7 %copy-start.34 = (f32[512]{0:T(512)}, f32[512]{0:T(512)S(1)}, u32[]{:S(2)}) copy-start(f32[512]{0:T(512)S(1)} %add_rsqrt_fusion.1) | copy-start | bytes 6148
  97.9 106.6 %all-to-all-start = ((bf16[512,3,1024]{0,1,2:T(4,128)(2,1)}), bf16[512,3,1024]{0,1,2:T(4,128)(2,1)}, u32[]{:S(2)}, u32[]{:S(2)}) async-start(bf16[512,3,1024]{0,1,2:T(4,128)(2,1)} %copy.72), calls=%async_computation | async-start | bytes 8388608 | tf_op jit(solution)/shard_map/all_to_all | solution.py:177
  103.0 254.6 %all-gather.12.cloned.1.call-start = ((), (), s32[]{:S(2)}) async-start(), calls=%async_computation.11 | async-start | bytes 8650752 | tf_op jit(solution)/shard_map/all_gather | solution.py:152
  216.3 59.3 %copy-start.43 = (bf16[128]{0:T(256)(128)(2,1)S(1)}, bf16[128]{0:T(256)(128)(2,1)}, u32[]{:S(2)}) copy-start(bf16[128]{0:T(256)(128)(2,1)} %param.30) | copy-start | bytes 772
  268.1 61.9 %all-to-all-start.1 = ((bf16[4,512,256]{1,2,0:T(8,128)(2,1)}), bf16[4,512,256]{1,2,0:T(8,128)(2,1)S(1)}, u32[]{:S(2)}, u32[]{:S(2)}) async-start(bf16[4,512,256]{1,2,0:T(8,128)(2,1)} %bitcast.12), calls=%async_computation.1 | async-start | bytes 2097152 | tf_op jit(solution)/shard_map/all_to_all | solution.py:187
  275.6 104.6 %copy-start.27 = (f32[1024]{0:T(1024)}, f32[1024]{0:T(1024)S(1)}, u32[]{:S(2)}) copy-start(f32[1024]{0:T(1024)S(1)} %convert_element_type.119) | copy-start | bytes 12292
  275.6 59.6 %copy-start.40 = (f32[1024]{0:T(1024)}, f32[1024]{0:T(1024)S(1)}, u32[]{:S(2)}) copy-start(f32[1024]{0:T(1024)S(1)} %convert_element_type.120) | copy-start | bytes 12292
  330.0 27.6 %copy-start.30 = (f32[32,1,128]{2,1,0:T(1,128)}, f32[32,1,128]{2,1,0:T(1,128)S(1)}, u32[]{:S(2)}) copy-start(f32[32,1,128]{2,1,0:T(1,128)S(1)} %convert_element_type.137) | copy-start | bytes 49156
  334.7 37.8 %copy-start.5 = (f32[512,1024]{1,0:T(8,128)}, f32[512,1024]{1,0:T(8,128)S(1)}, u32[]{:S(2)}) copy-start(f32[512,1024]{1,0:T(8,128)S(1)} %get-tuple-element.254) | copy-start | bytes 6291460
  334.7 45.5 %copy-start.19 = (f32[512]{0:T(512)}, f32[512]{0:T(512)S(1)}, u32[]{:S(2)}) copy-start(f32[512]{0:T(512)S(1)} %broadcast_multiply_fusion.4) | copy-start | bytes 6148
  335.1 45.1 %copy-start.32 = (f32[512]{0:T(512)}, f32[512]{0:T(512)S(1)}, u32[]{:S(2)}) copy-start(f32[512]{0:T(512)S(1)} %add_rsqrt_fusion) | copy-start | bytes 6148
  357.6 14.9 %copy-start.44 = (bf16[1024,4096]{1,0:T(8,128)(2,1)S(1)}, bf16[1024,4096]{1,0:T(8,128)(2,1)}, u32[]{:S(2)}) copy-start(bf16[1024,4096]{1,0:T(8,128)(2,1)} %all-gather.10.cloned.1.call-done) | copy-start | bytes 25165828
  385.9 27.0 %all-to-all-start.2 = ((bf16[512,4,256]{2,0,1:T(8,128)(2,1)}), bf16[512,4,256]{2,0,1:T(8,128)(2,1)}, u32[]{:S(2)}, u32[]{:S(2)}) async-start(bf16[512,4,256]{2,0,1:T(8,128)(2,1)} %bitcast.179), calls=%async_computation.2 | async-start | bytes 2097152 | tf_op jit(solution)/shard_map/all_to_all | solution.py:214
  390.4 414.4 %reduce-scatter.7.cloned.1.call-start = ((), (), s32[]{:S(2)}) async-start(), calls=%async_computation.13 | async-start | bytes 4325376 | tf_op jit(solution)/shard_map/reduce_scatter | solution.py:242
  397.2 455.8 %reduce-scatter.5.cloned.1.call-start = ((), (), s32[]{:S(2)}) async-start(), calls=%async_computation.12 | async-start | bytes 12976128 | tf_op jit(solution)/shard_map/reduce_scatter | solution.py:239
  696.5 345.6 %reduce-scatter.11.cloned.1.call-start = ((), (), s32[]{:S(2)}) async-start(), calls=%async_computation.15 | async-start | bytes 17301504 | tf_op jit(solution)/shard_map/reduce_scatter | solution.py:248
  714.0 515.6 %reduce-scatter.9.cloned.1.call-start = ((), (), s32[]{:S(2)}) async-start(), calls=%async_computation.14 | async-start | bytes 17301504 | tf_op jit(solution)/shard_map/reduce_scatter | solution.py:246
  741.5 59.7 %copy-start.4 = (f32[512,1024]{1,0:T(8,128)S(1)}, f32[512,1024]{1,0:T(8,128)}, u32[]{:S(2)}) copy-start(f32[512,1024]{1,0:T(8,128)} %copy-done.3) | copy-start | bytes 6291460
  (50 other events, 241.8 us)
Sparse Core Ops, SparseCore 0:
  10.8 70.8 all-gather.5
  84.6 102.7 all-gather.7
  190.2 78.1 all-gather.9
  271.1 86.4 all-gather.11
  397.4 115.2 reduce-scatter.6
  696.6 156.3 reduce-scatter.4
  855.9 186.1 reduce-scatter.10
  1044.9 184.6 reduce-scatter.8
where the time goes:
time: 1250 us; the launch traced here: 1240 us
  waiting for transfers between devices  577 us (46%)
  matrix products  282 us (23%)
  blocking collectives  238 us (19%)
  local copies, waits for them, and re-layouts  70.1 us (6%)
  other arithmetic  22.6 us (2%)
  starting transfers between devices  17.6 us (1%)
  between operations  14.8 us (1%)
  loops' own time  14 us (1%)
    reduce_scatter x1, waiting for transfers between devices, per_device(): lax.psum_scatter(g_w_back, ('seq', 'shard'), scatter_dimension=0, tiled=T...  189 us
    reduce_scatter x1, waiting for transfers between devices, per_device(): lax.psum_scatter(g_w_in, ('seq', 'shard'), scatter_dimension=0, tiled=True)  188 us
    all_to_all x1, waiting for transfers between devices, per_device(): lax.all_to_all(qkv.reshape(rows, 3, width), 'seq', split_axis=2, concat_a...  101 us
    all_to_all x1, blocking collectives, per_device(): lax.all_to_all(stacked, 'seq', split_axis=0, concat_axis=2, tiled=True)  97.2 us
    unnamed x2, blocking collectives  86.4 us
    all_gather x1, blocking collectives, per_device(): lax.all_gather(bias_in, ('seq', 'shard'), axis=0, tiled=True)  54.4 us
    reduce_scatter x1, waiting for transfers between devices, per_device(): lax.psum_scatter(g_w_qkv, ('seq', 'shard'), scatter_dimension=0, tiled=True)  48.2 us
    dot_general x4, matrix products, one_block(): jnp.einsum('qgd,kgd->gqk', do_blk, values, preferred_element_type=jnp.flo...  42 us
  transfers between devices with their start and end apart: 11, of which 7 were waited for; matrix products, arithmetic and copies ran while one was open for 28% of the time, Pallas kernels for 0%

commit v1 on v0

--- a/solution.py
+++ b/solution.py
@@ -7,6 +7,18 @@
 HEAD_DIM = 64
 norm_eps = 1e-05
 gelu_c = math.sqrt(2.0 / math.pi)
+
+
+def cut_along(shard, dim, size):
+    shape = shard.shape
+    blocks = shard.reshape(*shape[:dim], size, shape[dim] // size, *shape[dim + 1 :])
+    return jnp.moveaxis(blocks, dim, 0)
+
+
+def joined_along(blocks, dim):
+    lengths = list(blocks.shape[1:])
+    lengths[dim] *= blocks.shape[0]
+    return jnp.moveaxis(blocks, 0, dim).reshape(lengths)
 
 
 def normalize(values):
@@ -174,9 +186,15 @@
     h_one = (normed1 * g_one.astype(f32) + s_one.astype(f32)).astype(jnp.bfloat16)
     bias_qkv = jnp.concatenate([full_bq.astype(f32), jnp.zeros((width,), f32), full_bv.astype(f32)])
     qkv = (jnp.dot(h_one, full_qkv, preferred_element_type=f32) + bias_qkv).astype(jnp.bfloat16)
-    grouped = lax.all_to_all(
-        qkv.reshape(rows, 3, width), "seq", split_axis=2, concat_axis=0, tiled=True
-    )
+    x = qkv.reshape(rows, 3, width)
+    size, mine = (lax.axis_size("seq"), lax.axis_index("seq"))
+    pieces = cut_along(x, 2, size)
+    gathered = [pieces[mine]]
+    for step in range(1, size):
+        sent = pieces[mine ^ step]
+        gathered.append(lax.ppermute(sent, "seq", [(i, i ^ step) for i in range(size)]))
+    pieces = jnp.stack(gathered)[mine ^ jnp.arange(size)]
+    grouped = joined_along(pieces, 0)
     length = grouped.shape[0]
     local_width = grouped.shape[2]
     groups = local_width // HEAD_DIM

time: 1250 us -> 1230 us (0.984)
  waiting for transfers between devices: 577 us -> 552 us
    all_to_all x1 -> x0, waiting for transfers between devices: 101 us -> none  [per_device(): lax.all_to_all(qkv.reshape(rows, 3, width), 'seq', split_axis=2, concat_a...]
    ppermute x0 -> x3, waiting for transfers between devices: none -> 74 us  [per_device(): lax.ppermute(sent, 'seq', [(i, i ^ step) for i in range(size)])]
    another operation x2 -> x4, local copies, waits for them, and re-layouts: 2.15 us -> 15 us
  transfers between devices with their start and end apart: 11 -> 13, of which waited for: 7 -> 9; matrix products, arithmetic and copies ran while one was open for 28% -> 29% of each run, Pallas kernels for 0% -> 0%
where the time goes in v1:
time: 1230 us; the launch traced here: 1220 us
  waiting for transfers between devices  552 us (45%)
  matrix products  283 us (23%)
  blocking collectives  238 us (19%)
  local copies, waits for them, and re-layouts  75.2 us (6%)
  other arithmetic  24.5 us (2%)
  between operations  14.9 us (1%)
  loops' own time  14.5 us (1%)
  starting transfers between devices  13.4 us (1%)
    reduce_scatter x1, waiting for transfers between devices, per_device(): lax.psum_scatter(g_w_back, ('seq', 'shard'), scatter_dimension=0, tiled=T...  189 us
    reduce_scatter x1, waiting for transfers between devices, per_device(): lax.psum_scatter(g_w_in, ('seq', 'shard'), scatter_dimension=0, tiled=True)  188 us
    all_to_all x1, blocking collectives, per_device(): lax.all_to_all(stacked, 'seq', split_axis=0, concat_axis=2, tiled=True)  97.2 us
    unnamed x2, blocking collectives  86.3 us
    ppermute x3, waiting for transfers between devices, per_device(): lax.ppermute(sent, 'seq', [(i, i ^ step) for i in range(size)])  74 us
    all_gather x1, blocking collectives, per_device(): lax.all_gather(bias_in, ('seq', 'shard'), axis=0, tiled=True)  55 us
    reduce_scatter x1, waiting for transfers between devices, per_device(): lax.psum_scatter(g_w_qkv, ('seq', 'shard'), scatter_dimension=0, tiled=True)  48.3 us
    dot_general x4, matrix products, one_block(): jnp.einsum('qgd,kgd->gqk', do_blk, values, preferred_element_type=jnp.flo...  42.3 us
  transfers between devices with their start and end apart: 13, of which 9 were waited for; matrix products, arithmetic and copies ran while one was open for 29% of the time, Pallas kernels for 0%

profile of v1, /device:TPU:13, one launch (start us, length us, event | category | flops | bytes accessed | tf_op | source)
XLA Modules:
  0.0 1215.3 jit_solution(4173483604680152435)
XLA Ops:
  16.2 40.6 %all-reduce.18 = (bf16[1024]{0:T(1024)(128)(2,1)S(1)}, bf16[1024]{0:T(1024)(128)(2,1)S(1)}, bf16[1024]{0:T(1024)(128)(2,1)S(1)}, bf16[1024]{0:T(1024)(128)(2,1)S...) all-reduce(bf16[1024]{0:T(1024)(128)(2,1)S(1)} %dynamic-update-slic, ...), channel_id=1, replica_groups=mesh['seq'=4,'shard'=8] {'seq','shard'}, use_global_device_ids=true, to_apply=%add.3 | all-reduce | flops 8192 | bytes 32768
  60.0 21.7 %all-gather.6.cloned.1.call-done = bf16[1024,3072]{1,0:T(8,128)(2,1)} async-done(((bf16[32,3072]{1,0:T(8,128)(2,1)}), bf16[1024,3072]{1,0:T(8,128)(2,1)}) %all-gather.6.cloned.1.call-update) | async-done | bytes 6291472 | tf_op jit(solution)/shard_map/all_gather | solution.py:155
  108.9 38.0 %collective-permute-done.2 = bf16[512,3,256]{2,0,1:T(8,128)(2,1)S(1)} collective-permute-done((bf16[512,3,256]{2,0,1:T(8,128)(2,1)}, bf16[512,3,256]{2,0,1:T(8,128)(2,1)S(1)}, u32[]{:S(2)}, u32[]{:S(2)}) %collective-permute-start.2) | collective-permute-done | bytes 786464 | tf_op jit(solution)/shard_map/ppermute | solution.py:195
  148.7 34.2 %collective-permute-done.1 = bf16[512,3,256]{2,0,1:T(8,128)(2,1)} collective-permute-done((bf16[512,3,256]{2,0,1:T(8,128)(2,1)}, bf16[512,3,256]{2,0,1:T(8,128)(2,1)}, u32[]{:S(2)}, u32[]{:S(2)}) %collective-permute-start.1) | collective-permute-done | bytes 786464 | tf_op jit(solution)/shard_map/ppermute | solution.py:195
  193.4 51.3 %while.27 = (s32[]{:T(128)}, bf16[4,512,4,64]{1,3,2,0:T(8,128)(2,1)}, f32[4,4,512]{2,1,0:T(4,128)}, s32[4]{0:T(128)S(1)}, bf16[2048,4,64]{0,2,1:T(8,128)(2,1)S(1...) while((s32[]{:T(128)}, ...), condition=%wide.region_4.5_spmd, body=%wide.region_2.4_spmd.sunk | while | flops 1104280064 | bytes 43569372 | solution.py:76
  251.7 55.0 %all-gather = bf16[32,1,128]{2,1,0:T(2,128)(2,1)S(1)} all-gather(bf16[1,1,128]{2,1,0:T(2,128)(2,1)S(1)} %bitcast.202), channel_id=1, replica_groups=mesh['seq'=4,'shard'=8] {'seq','shard'}, dimensions={0}, use_global_device_ids=true | all-gather | bytes 8448 | tf_op jit(solution)/shard_map/all_gather | solution.py:163
  311.7 10.6 fusion.84
  322.3 13.4 %all-gather.12.cloned.1.call-done = bf16[4096,1024]{1,0:T(8,128)(2,1)} async-done(((bf16[128,1024]{1,0:T(8,128)(2,1)}), bf16[4096,1024]{1,0:T(8,128)(2,1)}) %all-gather.12.cloned.1.call-update) | async-done | bytes 8388624 | tf_op jit(solution)/shard_map/all_gather | solution.py:164
  335.7 15.0 %convert_reduce_fusion = (f32[4096]{0:T(1024)}, bf16[512,4096]{1,0:T(8,128)(2,1)}) fusion(f32[512,4096]{1,0:T(8,128)} %fusion.84, f32[4096]{0:T(1024)S(1)} %bitcast.199, bf16[4096,1024]{1,0:T(8,128)(2,1)} %all-gather.12.cloned.1.call-done, bf16[1,512,1024]{2,1,0:T(8,128)(2,1)} %param.33), kind=kOutput, calls=%fused_computation.53 | convolution fusion | flops 4341100544 | bytes 22052864 | tf_op jit(solution)/shard_map/dot_general | solution.py:129
  375.5 15.7 %all-to-all-done.1 = bf16[512,4,256]{2,0,1:T(8,128)(2,1)} async-done(((bf16[512,4,256]{2,0,1:T(8,128)(2,1)}), bf16[512,4,256]{2,0,1:T(8,128)(2,1)}, u32[]{:S(2)}, u32[]{:S(2)}) %all-to-all-start.1) | async-done | bytes 1048608 | tf_op jit(solution)/shard_map/all_to_all | solution.py:232
  395.0 156.4 %while.28 = (s32[]{:T(128)}, f32[2048,4,64]{0,2,1:T(8,128)}, f32[2048,4,64]{0,2,1:T(8,128)}, bf16[4,512,4,64]{1,3,2,0:T(8,128)(2,1)}, s32[4]{0:T(128)S(1)}, /*in...) while((s32[]{:T(128)}, f32[2048,4,64]{0,2,1:T(8,128)}, ...), condition=%wide.region_11.12_spmd.clone, body=%wide.region_9.11_spmd.clone.sunk | while | flops 2734291456 | bytes 138236336 | solution.py:112
  411.7 10.6 multiply_convert_fusion.5
  450.3 10.6 multiply_convert_fusion.5
  489.5 10.6 multiply_convert_fusion.5
  528.7 10.6 multiply_convert_fusion.5
  562.3 97.2 %all_to_all.50 = bf16[2048,3,256]{2,1,0:T(4,128)(2,1)S(1)} all-to-all(bf16[2048,3,256]{2,1,0:T(4,128)(2,1)} %copy.92), channel_id=1, replica_groups=mesh['seq'=4,'shard'=8] {'seq'}, dimensions={0} | all-to-all | bytes 6291456 | tf_op jit(solution)/shard_map/all_to_all | solution.py:244
  676.3 16.2 %fusion.68 = f32[4096,1024]{1,0:T(8,128)} fusion(bf16[1,512,1024]{2,1,0:T(8,128)(2,1)S(1)} %copy-done.17, f32[512,4096]{1,0:T(8,128)} %fusion.84, f32[4096]{0:T(1024)S(1)} %bitcast.200), kind=kOutput, calls=%fused_computation.100 | convolution fusion | flops 4315938816 | bytes 26230784 | tf_op jit(solution)/shard_map/dot_general | solution.py:123
  694.3 11.5 fusion.83
  706.5 13.2 %fusion.63 = bf16[1,512,1024]{2,1,0:T(8,128)(2,1)} fusion(f32[512,1024]{1,0:T(8,128)S(1)} %copy-done.6, bf16[4096,1024]{1,0:T(8,128)(2,1)} %all-gather.12.cloned.1.call-done, f32[1024]{0:T(1024)S(1)} %convert_element_type.124, f32[512,4096]{1,0:T(8,128)} %fusion.84, f32[4096]{0:T(1024)S(1)} %bitcast.201), kind=kOutput, calls=%fused_computation.96 | convolution fusion | flops 4317511680 | bytes 19943424 | tf_op jit(solution)/shard_map/dot_general | solution.py:215
  720.1 8.8 fusion.56
  728.9 45.7 %all-reduce.17 = (f32[1024]{0:T(1024)S(1)}, f32[1024]{0:T(1024)S(1)}, f32[1024]{0:T(1024)S(1)}, f32[1024]{0:T(1024)S(1)}, f32[1024]{0:T(1024)S(1)}, /*index=5*/f...) all-reduce(f32[1024]{0:T(1024)S(1)} %get-tuple-element.184, ...), channel_id=2, replica_groups=mesh['seq'=4,'shard'=8] {'seq','shard'}, use_global_device_ids=true, to_apply=%region_15.16.clone | all-reduce | flops 12288 | bytes 98304
  783.5 48.3 %reduce-scatter.5.cloned.1.call-done = f32[32,3072]{1,0:T(8,128)} async-done(((f32[1024,3072]{1,0:T(8,128)}), f32[32,3072]{1,0:T(8,128)}) %reduce-scatter.5.cloned.1.call-update) | async-done | bytes 393232 | tf_op jit(solution)/shard_map/reduce_scatter | solution.py:257
  831.7 189.0 %reduce-scatter.11.cloned.1.call-done = f32[128,1024]{1,0:T(8,128)} async-done(((f32[4096,1024]{1,0:T(8,128)}), f32[128,1024]{1,0:T(8,128)}) %reduce-scatter.11.cloned.1.call-update) | async-done | bytes 524304 | tf_op jit(solution)/shard_map/reduce_scatter | solution.py:266
  1020.8 187.5 %reduce-scatter.9.cloned.1.call-done = f32[32,4096]{1,0:T(8,128)} async-done(((f32[1024,4096]{1,0:T(8,128)}), f32[32,4096]{1,0:T(8,128)}) %reduce-scatter.9.cloned.1.call-update) | async-done | bytes 524304 | tf_op jit(solution)/shard_map/reduce_scatter | solution.py:264
  (311 shorter events, 282.1 us)
Async XLA Ops:
  7.2 74.5 %all-gather.6.cloned.1.call-start = ((), (), s32[]{:S(2)}) async-start(), calls=%async_computation.7 | async-start | bytes 6488064 | tf_op jit(solution)/shard_map/all_gather | solution.py:155
  7.9 298.8 %all-gather.8.cloned.1.call-start = ((), (), s32[]{:S(2)}) async-start(), calls=%async_computation.8 | async-start | bytes 2162688 | tf_op jit(solution)/shard_map/all_gather | solution.py:158
  8.7 303.1 %all-gather.10.cloned.1.call-start = ((), (), s32[]{:S(2)}) async-start(), calls=%async_computation.9 | async-start | bytes 8650752 | tf_op jit(solution)/shard_map/all_gather | solution.py:162
  9.4 326.3 %all-gather.12.cloned.1.call-start = ((), (), s32[]{:S(2)}) async-start(), calls=%async_computation.10 | async-start | bytes 8650752 | tf_op jit(solution)/shard_map/all_gather | solution.py:164
  56.8 24.9 %copy-start.28 = (f32[1024]{0:T(1024)}, f32[1024]{0:T(1024)S(1)}, u32[]{:S(2)}) copy-start(f32[1024]{0:T(1024)S(1)} %convert_element_type.112) | copy-start | bytes 12292
  106.1 40.9 %collective-permute-start.2 = (bf16[512,3,256]{2,0,1:T(8,128)(2,1)}, bf16[512,3,256]{2,0,1:T(8,128)(2,1)S(1)}, u32[]{:S(2)}, u32[]{:S(2)}) collective-permute-start(bf16[512,3,256]{2,0,1:T(8,128)(2,1)} %bitcast.144), channel_id=1, source_target_pairs={{0,24},{8,16},{16,8},{24,0},{1,25},{9,17},{17,9},{25,1},{2,26},{10... | collective-permute-start | bytes 2359304 | tf_op jit(solution)/shard_map/ppermute | solution.py:195
  106.6 42.1 %collective-permute-start = (bf16[512,3,256]{2,0,1:T(8,128)(2,1)}, bf16[512,3,256]{2,0,1:T(8,128)(2,1)S(1)}, u32[]{:S(2)}, u32[]{:S(2)}) collective-permute-start(bf16[512,3,256]{2,0,1:T(8,128)(2,1)} %bitcast.146), channel_id=1, source_target_pairs={{0,8},{8,0},{16,24},{24,16},{1,9},{9,1},{17,25},{25,17},{2,10},{10... | collective-permute-start | bytes 2359304 | tf_op jit(solution)/shard_map/ppermute | solution.py:195
  107.8 75.1 %collective-permute-start.1 = (bf16[512,3,256]{2,0,1:T(8,128)(2,1)}, bf16[512,3,256]{2,0,1:T(8,128)(2,1)}, u32[]{:S(2)}, u32[]{:S(2)}) collective-permute-start(bf16[512,3,256]{2,0,1:T(8,128)(2,1)} %bitcast.145), channel_id=1, source_target_pairs={{0,16},{8,24},{16,0},{24,8},{1,17},{9,25},{17,1},{25,9},{2,18},{10... | collective-permute-start | bytes 2359304 | tf_op jit(solution)/shard_map/ppermute | solution.py:195
  146.9 36.0 %copy-start.19 = (bf16[512,3,256]{2,0,1:T(8,128)(2,1)}, bf16[512,3,256]{2,0,1:T(8,128)(2,1)S(1)}, u32[]{:S(2)}) copy-start(bf16[512,3,256]{2,0,1:T(8,128)(2,1)S(1)} %collective-permute-done.2) | copy-start | bytes 2359300
  148.7 34.2 %copy-start.20 = (bf16[512,3,256]{2,0,1:T(8,128)(2,1)}, bf16[512,3,256]{2,0,1:T(8,128)(2,1)S(1)}, u32[]{:S(2)}) copy-start(bf16[512,3,256]{2,0,1:T(8,128)(2,1)S(1)} %collective-permute-done) | copy-start | bytes 2359300
  193.4 58.3 %copy-start.46 = (bf16[128]{0:T(256)(128)(2,1)S(1)}, bf16[128]{0:T(256)(128)(2,1)}, u32[]{:S(2)}) copy-start(bf16[128]{0:T(256)(128)(2,1)} %param.30) | copy-start | bytes 772
  245.6 61.1 %all-to-all-start = ((bf16[4,512,256]{1,2,0:T(8,128)(2,1)}), bf16[4,512,256]{1,2,0:T(8,128)(2,1)S(1)}, u32[]{:S(2)}, u32[]{:S(2)}) async-start(bf16[4,512,256]{1,2,0:T(8,128)(2,1)} %bitcast.17), calls=%async_computation | async-start | bytes 2097152 | tf_op jit(solution)/shard_map/all_to_all | solution.py:205
  251.7 106.7 %copy-start.30 = (f32[1024]{0:T(1024)}, f32[1024]{0:T(1024)S(1)}, u32[]{:S(2)}) copy-start(f32[1024]{0:T(1024)S(1)} %convert_element_type.119) | copy-start | bytes 12292
  251.7 60.1 %copy-start.43 = (f32[1024]{0:T(1024)}, f32[1024]{0:T(1024)S(1)}, u32[]{:S(2)}) copy-start(f32[1024]{0:T(1024)S(1)} %convert_element_type.120) | copy-start | bytes 12292
  306.7 29.0 %copy-start.33 = (f32[32,1,128]{2,1,0:T(1,128)}, f32[32,1,128]{2,1,0:T(1,128)S(1)}, u32[]{:S(2)}) copy-start(f32[32,1,128]{2,1,0:T(1,128)S(1)} %convert_element_type.137) | copy-start | bytes 49156
  311.3 39.4 %copy-start.5 = (f32[512,1024]{1,0:T(8,128)}, f32[512,1024]{1,0:T(8,128)S(1)}, u32[]{:S(2)}) copy-start(f32[512,1024]{1,0:T(8,128)S(1)} %get-tuple-element.258) | copy-start | bytes 6291460
  311.3 47.1 %copy-start.22 = (f32[512]{0:T(512)}, f32[512]{0:T(512)S(1)}, u32[]{:S(2)}) copy-start(f32[512]{0:T(512)S(1)} %broadcast_multiply_fusion.4) | copy-start | bytes 6148
  311.7 46.7 %copy-start.35 = (f32[512]{0:T(512)}, f32[512]{0:T(512)S(1)}, u32[]{:S(2)}) copy-start(f32[512]{0:T(512)S(1)} %add_rsqrt_fusion) | copy-start | bytes 6148
  364.2 27.0 %all-to-all-start.1 = ((bf16[512,4,256]{2,0,1:T(8,128)(2,1)}), bf16[512,4,256]{2,0,1:T(8,128)(2,1)}, u32[]{:S(2)}, u32[]{:S(2)}) async-start(bf16[512,4,256]{2,0,1:T(8,128)(2,1)} %bitcast.190), calls=%async_computation.1 | async-start | bytes 2097152 | tf_op jit(solution)/shard_map/all_to_all | solution.py:232
  368.6 414.8 %reduce-scatter.7.cloned.1.call-start = ((), (), s32[]{:S(2)}) async-start(), calls=%async_computation.12 | async-start | bytes 4325376 | tf_op jit(solution)/shard_map/reduce_scatter | solution.py:260
  375.5 456.2 %reduce-scatter.5.cloned.1.call-start = ((), (), s32[]{:S(2)}) async-start(), calls=%async_computation.11 | async-start | bytes 12976128 | tf_op jit(solution)/shard_map/reduce_scatter | solution.py:257
  675.1 345.6 %reduce-scatter.11.cloned.1.call-start = ((), (), s32[]{:S(2)}) async-start(), calls=%async_computation.14 | async-start | bytes 17301504 | tf_op jit(solution)/shard_map/reduce_scatter | solution.py:266
  692.6 515.7 %reduce-scatter.9.cloned.1.call-start = ((), (), s32[]{:S(2)}) async-start(), calls=%async_computation.13 | async-start | bytes 17301504 | tf_op jit(solution)/shard_map/reduce_scatter | solution.py:264
  720.1 59.7 %copy-start.4 = (f32[512,1024]{1,0:T(8,128)S(1)}, f32[512,1024]{1,0:T(8,128)}, u32[]{:S(2)}) copy-start(f32[512,1024]{1,0:T(8,128)} %copy-done.3) | copy-start | bytes 6291460
  (55 other events, 332.8 us)
Sparse Core Ops, SparseCore 0:
  10.8 70.8 all-gather.5
  84.6 82.9 all-gather.7
  170.4 80.8 all-gather.9
  254.1 81.5 all-gather.11
  375.6 115.2 reduce-scatter.6
  675.2 156.4 reduce-scatter.4
  834.6 186.1 reduce-scatter.10
  1023.6 184.6 reduce-scatter.8
